TPU v7x, 32 devices: a whole 2x2x4 slice. The times are simulated.
32 devices in a mesh: sp: 4 (over z), tp: 8 (over y, x, core).
Axes of the slice: x: 2, y: 2, z: 4, core: 2. Of those that a mesh axis runs over, the one named last changes fastest.
Arguments:
- tokens: bfloat16 [8192, 2048], P(('sp', 'tp')), may hold values from -3 to 3
- queries: bfloat16 [8192, 2048], P(('sp', 'tp')), may hold values from -140 to 140
- keys: bfloat16 [8192, 1024], P(('sp', 'tp')), may hold values from -6 to 6
- values: bfloat16 [8192, 1024], P(('sp', 'tp')), may hold values from -6 to 6
- out_weight: bfloat16 [2048, 2048], P('sp', 'tp'), may hold values from -0.25 to 0.25
- norm_gain: bfloat16 [2048], replicated, may hold values from 0.099609375 to 1.8984375
- gate_weight: bfloat16 [2048, 7168], P('sp', 'tp'), may hold values from -0.125 to 0.125
- up_weight: bfloat16 [2048, 7168], P('sp', 'tp'), may hold values from -0.125 to 0.125
- down_weight: bfloat16 [7168, 2048], P('tp', 'sp'), may hold values from -0.125 to 0.125
Outputs:
- attended: bfloat16 [8192, 2048], P(('sp', 'tp'))
- layer_out: bfloat16 [8192, 2048], P(('sp', 'tp'))
All inputs are finite; a program needn't handle non-finite values.
Results may differ from a plain program's by a relative error of at most 0.023.
Values may be sent and summed in bfloat16 or wider, within the bound.
A program may use at most 256 MiB of HBM per device.

v0:
```python
import jax
import jax.numpy as jnp
from jax import lax
from jax.sharding import PartitionSpec as P

HEAD_DIM = 128
norm_eps = 1e-05


def attend(q_block, query_pos, k_block, v_block, key_pos, kv_local):
    row_count = q_block.shape[0]
    key_count = k_block.shape[0]
    q_four = q_block.reshape(row_count, kv_local, -1, HEAD_DIM)
    k_three = k_block.reshape(key_count, kv_local, HEAD_DIM)
    v_three = v_block.reshape(key_count, kv_local, HEAD_DIM)
    scores = jnp.einsum(
        "qhgd,khd->hgqk", q_four, k_three, preferred_element_type=jnp.float32
    ) * HEAD_DIM ** (-0.5)
    causal = key_pos[None, :] <= query_pos[:, None]
    scores = jnp.where(causal[None, None, :, :], scores, -1e30)
    row_peak = jnp.max(scores, axis=-1, keepdims=True)
    exp_terms = jnp.exp(scores - row_peak)
    probs = (exp_terms / jnp.sum(exp_terms, axis=-1, keepdims=True)).astype(jnp.bfloat16)
    mixed_out = jnp.einsum("hgqk,khd->qhgd", probs, v_three, preferred_element_type=jnp.float32)
    return mixed_out.astype(jnp.bfloat16).reshape(row_count, -1)


def add_rows(all_rows, weight_piece):
    return jnp.dot(all_rows, weight_piece, preferred_element_type=jnp.float32)


def shards(
    tokens, queries, keys, values, out_weight, norm_gain, gate_weight, up_weight, down_weight
):
    shard_rows = tokens.shape[0]
    sp_count = lax.axis_size("sp")
    tp_count = lax.axis_size("tp")
    segment_len = shard_rows * tp_count
    seq_len = segment_len * sp_count
    local_q = lax.all_to_all(queries, "sp", split_axis=1, concat_axis=0, tiled=True)
    part_keys, part_values = (
        lax.all_to_all(keys, "sp", split_axis=1, concat_axis=0, tiled=True),
        lax.all_to_all(values, "sp", split_axis=1, concat_axis=0, tiled=True),
    )
    width_kv = part_keys.shape[1]
    grid_keys, grid_values = (
        lax.all_gather(part_keys.reshape(sp_count, shard_rows, width_kv), "tp", axis=1, tiled=True),
        lax.all_gather(
            part_values.reshape(sp_count, shard_rows, width_kv), "tp", axis=1, tiled=True
        ),
    )
    all_keys = grid_keys.reshape(seq_len, width_kv)
    all_values = grid_values.reshape(seq_len, width_kv)
    kv_local = all_keys.shape[1] // HEAD_DIM
    query_index = jnp.arange(sp_count * shard_rows, dtype=jnp.int32)
    query_pos = (
        query_index // shard_rows * segment_len
        + lax.axis_index("tp") * shard_rows
        + query_index % shard_rows
    )
    key_pos = jnp.arange(seq_len, dtype=jnp.int32)
    pieces_out = []
    for segment in range(sp_count):
        first_row = segment * shard_rows
        key_reach = (segment + 1) * segment_len
        pieces_out.append(
            attend(
                local_q[first_row : first_row + shard_rows],
                query_pos[first_row : first_row + shard_rows],
                all_keys[:key_reach],
                all_values[:key_reach],
                key_pos[:key_reach],
                kv_local,
            )
        )
    attn = jnp.concatenate(pieces_out, axis=0)
    wo_full = lax.all_gather(out_weight, "tp", axis=1, tiled=True)
    block_rows = attn
    attn_part = lax.psum_scatter(
        jnp.dot(block_rows, wo_full, preferred_element_type=jnp.float32).astype(jnp.bfloat16),
        "sp",
        scatter_dimension=0,
        tiled=True,
    ).astype(jnp.float32)
    attended = (tokens.astype(jnp.float32) + attn_part).astype(jnp.bfloat16)
    attended_wide = attended.astype(jnp.float32)
    inverse_rms = lax.rsqrt(
        jnp.mean(attended_wide * attended_wide, axis=1, keepdims=True) + norm_eps
    )
    normed = (attended_wide * inverse_rms * norm_gain.astype(jnp.float32)).astype(jnp.bfloat16)
    all_rows = lax.all_gather(normed, "tp", axis=0, tiled=True)

    def add_single(weight_piece):
        return add_rows(all_rows, weight_piece)

    gate_sum = add_single(lax.all_gather(gate_weight, "sp", axis=0, tiled=True))
    up_sum = add_single(lax.all_gather(up_weight, "sp", axis=0, tiled=True))
    hidden = (jax.nn.silu(gate_sum) * up_sum).astype(jnp.bfloat16)
    down_full = lax.all_gather(down_weight, "sp", axis=1, tiled=True)
    block_rows = hidden
    ffn_part = lax.psum_scatter(
        jnp.dot(block_rows, down_full, preferred_element_type=jnp.float32).astype(jnp.bfloat16),
        "tp",
        scatter_dimension=0,
        tiled=True,
    ).astype(jnp.float32)
    layer_out = (attended_wide + ffn_part).astype(jnp.bfloat16)
    return (attended, layer_out)


def solution(mesh):
    return jax.shard_map(
        shards,
        mesh=mesh,
        in_specs=(
            P(("sp", "tp"), None),
            P(("sp", "tp"), None),
            P(("sp", "tp"), None),
            P(("sp", "tp"), None),
            P("sp", "tp"),
            P(),
            P("sp", "tp"),
            P("sp", "tp"),
            P("tp", "sp"),
        ),
        out_specs=(P(("sp", "tp"), None), P(("sp", "tp"), None)),
        check_vma=False,
    )
```

profile of v0, /device:TPU:0, one launch (start us, length us, event | category | flops | bytes accessed | tf_op | source)
XLA Modules:
  0.0 878.5 jit_solution(10126609819446409011)
XLA Ops:
  8.5 20.7 %all_to_all.48 = bf16[256,4,256]{0,2,1:T(8,128)(2,1)} all-to-all(bf16[256,4,256]{0,2,1:T(8,128)(2,1)S(1)} %bitcast.109), channel_id=1, replica_groups=mesh['sp'=4,'tp'=8] {'sp'}, dimensions={1} | all-to-all | bytes 1048576 | tf_op jit(solution)/shard_map/all_to_all | solution.py:42
  30.4 16.8 %all_to_all.49 = bf16[256,4,256]{2,0,1:T(8,128)(2,1)} all-to-all(bf16[256,4,256]{2,0,1:T(8,128)(2,1)S(1)} %bitcast.110), channel_id=1, replica_groups=mesh['sp'=4,'tp'=8] {'sp'}, dimensions={1} | all-to-all | bytes 1048576 | tf_op jit(solution)/shard_map/all_to_all | solution.py:43
  64.0 13.7 %all-to-all-done.1 = bf16[256,4,512]{0,2,1:T(8,128)(2,1)S(1)} async-done(((bf16[256,4,512]{0,2,1:T(8,128)(2,1)}), bf16[256,4,512]{0,2,1:T(8,128)(2,1)S(1)}, u32[]{:S(2)}, u32[]{:S(2)}) %all-to-all-start.1) | async-done | bytes 1048608 | tf_op jit(solution)/shard_map/all_to_all | solution.py:40
  124.2 18.2 %fusion.15 = f32[2,8192,256,2]{2,1,3,0:T(8,128)} fusion(bf16[256,2,2,128]{0,3,2,1:T(8,128)(2,1)} %bitcast.113, bf16[8192,2,128,1]{2,1,0,3:T(2,128)(2,1)} %bitcast.100), kind=kOutput, calls=%fused_computation.30 | convolution fusion | flops 2147483648 | bytes 38010880 | tf_op jit(solution)/shard_map/qhgd,khd->hgqk/dot_general | solution.py:16
  142.4 10.1 %fusion.23 = f32[2,6144,256,2]{2,1,3,0:T(8,128)} fusion(bf16[256,2,2,128]{0,3,2,1:T(8,128)(2,1)S(1)} %bitcast.112, bf16[6144,2,128,1]{2,1,0,3:T(2,128)(2,1)S(1)} %bitcast.101), kind=kOutput, calls=%fused_computation.39 | convolution fusion | flops 1610612736 | bytes 28573696 | tf_op jit(solution)/shard_map/qhgd,khd->hgqk/dot_general | solution.py:16
  152.4 8.1 fusion.30
  160.5 18.3 %fusion.71 = (f32[2,2,256]{2,1,0:T(2,128)S(1)}, f32[2,2,256,4096]{2,3,1,0:T(8,128)}) fusion(f32[2,4096,256,2]{2,1,3,0:T(8,128)} %fusion.30, pred[256,4096]{0,1:T(8,128)(4,1)S(1)} %copy-done.6), kind=kOutput, calls=%fused_computation.96 | output fusion | flops 25169920 | bytes 34607104 | tf_op jit(solution)/shard_map/sub | solution.py:22
  181.8 10.5 %broadcast_in_dim.53 = f32[2,2,256,6144]{2,3,1,0:T(8,128)} broadcast(f32[]{:T(128)} %constant.50.clone.1), dimensions={} | broadcast | bytes 25165828 | tf_op jit(solution)/shard_map/jit(_where)/broadcast_in_dim | solution.py:20
  192.3 10.5 %mul.80 = f32[2,6144,256,2]{2,1,3,0:T(8,128)} broadcast(f32[]{:T(128)} %constant.49.clone.1), dimensions={} | broadcast | bytes 25165828 | tf_op jit(solution)/shard_map/mul | solution.py:16
  202.8 56.1 %fusion.70 = (f32[2,2,256]{2,1,0:T(2,128)S(1)}, f32[2,2,256,6144]{2,3,1,0:T(8,128)}) fusion(pred[2,2,256,6144]{2,3,1,0:T(8,128)(4,1)S(1)} %broadcast_in_dim.52, f32[2,2,256,6144]{2,3,1,0:T(8,128)} %broadcast_in_dim.53, f32[2,6144,256,2]{2,1,3,0:T(8,128)} %fusion.23, f32[2,6144,256,2]{2,1,3,0:T(8,128)} %mul.80), kind=kOutput, calls=%fused_computation.95 | output fusion | flops 37754880 | bytes 106958848 | tf_op jit(solution)/shard_map/sub | solution.py:22
  258.9 11.8 %fusion.36 = bf16[2,2,256,128]{2,3,1,0:T(8,128)(2,1)} fusion(f32[2,2,256,6144]{2,3,1,0:T(8,128)} %get-tuple-element.15, f32[2,2,256]{2,1,0:T(2,128)S(1)} %get-tuple-element.14, bf16[6144,2,128,1]{2,1,0,3:T(2,128)(2,1)} %bitcast.105), kind=kOutput, calls=%fused_computation.56 | convolution fusion | flops 1623326720 | bytes 28577792 | tf_op jit(solution)/shard_map/hgqk,khd->qhgd/dot_general | solution.py:24
  270.7 8.2 fusion.33
  290.5 11.1 %broadcast_in_dim.77 = f32[2,2,256,8192]{2,3,1,0:T(8,128)} broadcast(f32[]{:T(128)} %constant.50.clone.1), dimensions={} | broadcast | bytes 33554436 | tf_op jit(solution)/shard_map/jit(_where)/broadcast_in_dim | solution.py:20
  301.7 11.0 %mul.83 = f32[2,8192,256,2]{2,1,3,0:T(8,128)} broadcast(f32[]{:T(128)} %constant.49.clone.1), dimensions={} | broadcast | bytes 33554436 | tf_op jit(solution)/shard_map/mul | solution.py:16
  312.6 78.0 %fusion.69 = (f32[2,2,256]{2,1,0:T(2,128)S(1)}, f32[2,2,256,8192]{2,3,1,0:T(8,128)}) fusion(pred[2,2,256,8192]{2,3,1,0:T(8,128)(4,1)} %broadcast_in_dim.76, f32[2,2,256,8192]{2,3,1,0:T(8,128)} %broadcast_in_dim.77, f32[2,8192,256,2]{2,1,3,0:T(8,128)} %fusion.15, f32[2,8192,256,2]{2,1,3,0:T(8,128)} %mul.83), kind=kOutput, calls=%fused_computation.94 | output fusion | flops 50339840 | bytes 142610432 | tf_op jit(solution)/shard_map/sub | solution.py:22
  401.7 13.5 %fusion.39 = bf16[2,2,256,128]{2,3,1,0:T(8,128)(2,1)S(1)} fusion(f32[2,2,256,8192]{2,3,1,0:T(8,128)} %get-tuple-element.13, f32[2,2,256]{2,1,0:T(2,128)S(1)} %get-tuple-element.12, bf16[8192,2,128,1]{2,1,0,3:T(2,128)(2,1)} %bitcast.103), kind=kOutput, calls=%fused_computation.57 | convolution fusion | flops 2164391936 | bytes 38014976 | tf_op jit(solution)/shard_map/hgqk,khd->qhgd/dot_general | solution.py:24
  422.0 76.5 %reduce-scatter.3.cloned.1.call-done = bf16[256,2048]{1,0:T(8,128)(2,1)} async-done(((bf16[1024,2048]{1,0:T(8,128)(2,1)}), bf16[256,2048]{1,0:T(8,128)(2,1)}) %reduce-scatter.3.cloned.1.call-update) | async-done | bytes 1048592 | tf_op jit(solution)/shard_map/reduce_scatter | solution.py:79
  503.1 69.4 %all-gather.16.cloned.1.call-done = bf16[2048,896]{1,0:T(8,128)(2,1)} async-done(((bf16[512,896]{1,0:T(8,128)(2,1)}), bf16[2048,896]{1,0:T(8,128)(2,1)}) %all-gather.16.cloned.1.call-update) | async-done | bytes 3670032 | tf_op jit(solution)/shard_map/all_gather | solution.py:96
  572.5 55.2 %all-gather.14.cloned.1.call-done = bf16[2048,2048]{1,0:T(8,128)(2,1)} async-done(((bf16[256,2048]{1,0:T(8,128)(2,1)}), bf16[2048,2048]{1,0:T(8,128)(2,1)}) %all-gather.14.cloned.1.call-update) | async-done | bytes 8388624 | tf_op jit(solution)/shard_map/all_gather | solution.py:91
  627.7 14.1 %fusion.73 = f32[2048,896]{1,0:T(8,128)} fusion(bf16[2048,2048]{1,0:T(8,128)(2,1)} %all-gather.14.cloned.1.call-done, bf16[2048,896]{1,0:T(8,128)(2,1)} %all-gather.16.cloned.1.call-done), kind=kOutput, calls=%fused_computation.98 | convolution fusion | flops 7516192768 | bytes 19398656 | tf_op jit(solution)/shard_map/dot_general | solution.py:29
  641.8 59.6 %all-gather.20.cloned.1.call-done = bf16[896,2048]{1,0:T(8,128)(2,1)} async-done(((bf16[896,512]{1,0:T(8,128)(2,1)}), bf16[896,2048]{1,0:T(8,128)(2,1)}) %all-gather.20.cloned.1.call-update) | async-done | bytes 3670032 | tf_op jit(solution)/shard_map/all_gather | solution.py:99
  701.4 72.3 %all-gather.18.cloned.1.call-done = bf16[2048,896]{1,0:T(8,128)(2,1)} async-done(((bf16[512,896]{1,0:T(8,128)(2,1)}), bf16[2048,896]{1,0:T(8,128)(2,1)}) %all-gather.18.cloned.1.call-update) | async-done | bytes 3670032 | tf_op jit(solution)/shard_map/all_gather | solution.py:97
  773.6 25.3 %convolution_convert_fusion = bf16[2048,2048]{1,0:T(8,128)(2,1)} fusion(bf16[896,2048]{1,0:T(8,128)(2,1)} %all-gather.20.cloned.1.call-done, f32[2048,896]{1,0:T(8,128)} %fusion.73, bf16[2048,2048]{1,0:T(8,128)(2,1)} %all-gather.14.cloned.1.call-done, bf16[2048,896]{1,0:T(8,128)(2,1)} %all-gather.18.cloned.1.call-done), kind=kOutput, calls=%fused_computation.26 | convolution fusion | flops 15047589888 | bytes 31457280 | tf_op jit(solution)/shard_map/dot_general | solution.py:102
  799.0 70.2 %reduce-scatter.5.cloned.1.call-done = bf16[256,2048]{1,0:T(8,128)(2,1)} async-done(((bf16[2048,2048]{1,0:T(8,128)(2,1)}), bf16[256,2048]{1,0:T(8,128)(2,1)}) %reduce-scatter.5.cloned.1.call-update) | async-done | bytes 1048592 | tf_op jit(solution)/shard_map/reduce_scatter | solution.py:101
  (92 shorter events, 105.2 us)
Async XLA Ops:
  7.2 71.5 %all-gather.8.cloned.1.call-start = ((), (), s32[]{:S(2)}) async-start(), calls=%async_computation.5 | async-start | bytes 4718592 | tf_op jit(solution)/shard_map/all_gather | solution.py:47
  29.2 75.1 %all-gather.10.cloned.1.call-start = ((), (), s32[]{:S(2)}) async-start(), calls=%async_computation.6 | async-start | bytes 4718592 | tf_op jit(solution)/shard_map/all_gather | solution.py:48
  49.4 28.3 %all-to-all-start.1 = ((bf16[256,4,512]{0,2,1:T(8,128)(2,1)}), bf16[256,4,512]{0,2,1:T(8,128)(2,1)S(1)}, u32[]{:S(2)}, u32[]{:S(2)}) async-start(bf16[256,4,512]{0,2,1:T(8,128)(2,1)} %bitcast.4), calls=%async_computation.1 | async-start | bytes 2097152 | tf_op jit(solution)/shard_map/all_to_all | solution.py:40
  53.0 362.3 %all-gather.12.cloned.1.call-start = ((), (), s32[]{:S(2)}) async-start(), calls=%async_computation.7 | async-start | bytes 2359296 | tf_op jit(solution)/shard_map/all_gather | solution.py:77
  53.7 444.7 %reduce-scatter.3.cloned.1.call-start = ((), (), s32[]{:S(2)}) async-start(), calls=%async_computation.8 | async-start | bytes 5242880 | tf_op jit(solution)/shard_map/reduce_scatter | solution.py:79
  84.8 7.2 slice-start.3
  112.5 8.2 slice-start.1
  124.2 18.2 %copy-start = (bf16[6144,2,128]{2,1,0:T(2,128)(2,1)S(1)}, bf16[6144,2,128]{2,1,0:T(2,128)(2,1)}, u32[]{:S(2)}) copy-start(bf16[6144,2,128]{2,1,0:T(2,128)(2,1)} %reshape.205) | copy-start | bytes 9437188
  124.2 18.2 %copy-start.5 = (bf16[1,256,512]{1,2,0:T(8,128)(2,1)S(1)}, bf16[1,256,512]{1,2,0:T(8,128)(2,1)}, u32[]{:S(2)}) copy-start(bf16[1,256,512]{1,2,0:T(8,128)(2,1)} %get-tuple-element.6) | copy-start | bytes 786436
  142.4 10.1 %copy-start.3 = (bf16[4096,2,128]{2,1,0:T(2,128)(2,1)S(1)}, bf16[4096,2,128]{2,1,0:T(2,128)(2,1)}, u32[]{:S(2)}) copy-start(bf16[4096,2,128]{2,1,0:T(2,128)(2,1)} %reshape.201) | copy-start | bytes 6291460
  152.4 8.1 copy-start.6
  258.9 11.8 %copy-start.4 = (bf16[4096,2,128]{2,1,0:T(2,128)(2,1)S(1)}, bf16[4096,2,128]{2,1,0:T(2,128)(2,1)}, u32[]{:S(2)}) copy-start(bf16[4096,2,128]{2,1,0:T(2,128)(2,1)} %reshape.219) | copy-start | bytes 6291460
  270.7 8.2 slice-start.4
  270.7 8.2 copy-start.9
  312.6 78.0 %copy-start.8 = (bf16[1,2048,256]{1,2,0:T(8,128)(2,1)S(1)}, bf16[1,2048,256]{1,2,0:T(8,128)(2,1)}, u32[]{:S(2)}) copy-start(bf16[1,2048,256]{1,2,0:T(8,128)(2,1)} %copy.24) | copy-start | bytes 3145732
  401.7 13.6 %copy-start.11 = (bf16[2,2,256,128]{2,3,1,0:T(8,128)(2,1)S(1)}, bf16[2,2,256,128]{2,3,1,0:T(8,128)(2,1)}, u32[]{:S(2)}) copy-start(bf16[2,2,256,128]{2,3,1,0:T(8,128)(2,1)} %fusion.36) | copy-start | bytes 786436
  401.7 13.6 %copy-start.12 = (bf16[2,2,256,128]{2,3,1,0:T(8,128)(2,1)S(1)}, bf16[2,2,256,128]{2,3,1,0:T(8,128)(2,1)}, u32[]{:S(2)}) copy-start(bf16[2,2,256,128]{2,3,1,0:T(8,128)(2,1)} %fusion.33) | copy-start | bytes 786436
  415.3 83.2 %copy-start.7 = (bf16[256,2048]{1,0:T(8,128)(2,1)S(1)}, bf16[256,2048]{1,0:T(8,128)(2,1)}, u32[]{:S(2)}) copy-start(bf16[256,2048]{1,0:T(8,128)(2,1)} %param.9) | copy-start | bytes 3145732
  421.3 151.2 %all-gather.16.cloned.1.call-start = ((), (), s32[]{:S(2)}) async-start(), calls=%async_computation.10 | async-start | bytes 4587520 | tf_op jit(solution)/shard_map/all_gather | solution.py:96
  421.9 205.8 %all-gather.14.cloned.1.call-start = ((), (), s32[]{:S(2)}) async-start(), calls=%async_computation.9 | async-start | bytes 9437184 | tf_op jit(solution)/shard_map/all_gather | solution.py:91
  500.2 369.0 %copy-start.1 = (bf16[256,2048]{1,0:T(8,128)(2,1)}, bf16[256,2048]{1,0:T(8,128)(2,1)S(1)}, u32[]{:S(2)}) copy-start(bf16[256,2048]{1,0:T(8,128)(2,1)S(1)} %get-tuple-element.3) | copy-start | bytes 3145732
  501.5 199.8 %all-gather.20.cloned.1.call-start = ((), (), s32[]{:S(2)}) async-start(), calls=%async_computation.12 | async-start | bytes 4587520 | tf_op jit(solution)/shard_map/all_gather | solution.py:99
  502.3 271.4 %all-gather.18.cloned.1.call-start = ((), (), s32[]{:S(2)}) async-start(), calls=%async_computation.11 | async-start | bytes 4587520 | tf_op jit(solution)/shard_map/all_gather | solution.py:97
  503.0 366.2 %reduce-scatter.5.cloned.1.call-start = ((), (), s32[]{:S(2)}) async-start(), calls=%async_computation.13 | async-start | bytes 9437184 | tf_op jit(solution)/shard_map/reduce_scatter | solution.py:101
  (4 other events, 21.0 us)
Sparse Core Ops, SparseCore 0:
  29.3 36.4 all-gather.7
  67.7 36.5 all-gather.9
  106.2 28.0 all-gather.11
  421.4 76.9 reduce-scatter.2
  499.9 72.5 all-gather.15
  574.8 52.8 all-gather.13
  629.3 72.0 all-gather.19
  702.9 70.6 all-gather.17
  799.1 70.0 reduce-scatter.4
where the time goes:
time: 882 us; the launch traced here: 879 us
  waiting for transfers between devices  424 us (48%)
  other arithmetic  168 us (19%)
  matrix products  126 us (14%)
  local copies, waits for them, and re-layouts  105 us (12%)
  blocking collectives  37.5 us (4%)
  between operations  14.2 us (2%)
    sub x3, other arithmetic, attend(): exp_terms = jnp.exp(scores - row_peak)  152 us
    reduce_scatter x1, waiting for transfers between devices, shards(): lax.psum_scatter(jnp.dot(block_rows, wo_full, preferred_element_type=jnp....  76.5 us
    all_gather x1, waiting for transfers between devices, shards(): up_sum = add_single(lax.all_gather(up_weight, 'sp', axis=0, tiled=True))  72.3 us
    reduce_scatter x1, waiting for transfers between devices, shards(): lax.psum_scatter(jnp.dot(block_rows, down_full, preferred_element_type=jn...  70.2 us
    all_gather x1, waiting for transfers between devices, shards(): gate_sum = add_single(lax.all_gather(gate_weight, 'sp', axis=0, tiled=True))  69.4 us
    all_gather x1, waiting for transfers between devices, shards(): down_full = lax.all_gather(down_weight, 'sp', axis=1, tiled=True)  59.6 us
    all_gather x1, waiting for transfers between devices, shards(): all_rows = lax.all_gather(normed, 'tp', axis=0, tiled=True)  55.2 us
    dot_general x4, matrix products, attend(): jnp.einsum('hgqk,khd->qhgd', probs, v_three, preferred_element_type=jnp.f...  37.6 us
  transfers between devices with their start and end apart: 10, of which 8 were waited for; matrix products, arithmetic and copies ran while one was open for 41% of the time, Pallas kernels for 0%

commit v1 on v0

--- a/solution.py
+++ b/solution.py
@@ -88,7 +88,12 @@
         jnp.mean(attended_wide * attended_wide, axis=1, keepdims=True) + norm_eps
     )
     normed = (attended_wide * inverse_rms * norm_gain.astype(jnp.float32)).astype(jnp.bfloat16)
-    all_rows = lax.all_gather(normed, "tp", axis=0, tiled=True)
+    ring = [normed]
+    for hop in range(7):
+        ring.append(lax.ppermute(ring[-1], "tp", [(dev, (dev + 1) % 8) for dev in range(8)]))
+    all_rows = jnp.roll(
+        jnp.concatenate(ring[::-1], axis=0), (lax.axis_index("tp") + 1) * ring[0].shape[0], axis=0
+    )
 
     def add_single(weight_piece):
         return add_rows(all_rows, weight_piece)

time: 882 us -> 826 us (0.937)
  waiting for transfers between devices: 424 us -> 339 us
  local copies, waits for them, and re-layouts: 105 us -> 131 us
    ppermute x0 -> x7, waiting for transfers between devices: none -> 106 us  [shards(): lax.ppermute(ring[-1], 'tp', [(dev, (dev + 1) % 8) for dev in range(8)])]
    all_gather x1, waiting for transfers between devices: 72.3 us -> 0.01 us  [shards(): up_sum = add_single(lax.all_gather(up_weight, 'sp', axis=0, tiled=True))]
    all_gather x1, waiting for transfers between devices: 59.6 us -> 0.01 us  [shards(): down_full = lax.all_gather(down_weight, 'sp', axis=1, tiled=True)]
    all_gather x1 -> x0, waiting for transfers between devices: 55.2 us -> none  [shards(): all_rows = lax.all_gather(normed, 'tp', axis=0, tiled=True)]
    unnamed x28 -> x54, local copies, waits for them, and re-layouts: 3.56 us -> 29.3 us
  transfers between devices with their start and end apart: 10 -> 16, of which waited for: 8 -> 12; matrix products, arithmetic and copies ran while one was open for 41% -> 47% of each run, Pallas kernels for 0% -> 0%
where the time goes in v1:
time: 826 us; the launch traced here: 822 us
  waiting for transfers between devices  339 us (41%)
  other arithmetic  170 us (21%)
  local copies, waits for them, and re-layouts  131 us (16%)
  matrix products  126 us (15%)
  blocking collectives  37.5 us (5%)
  between operations  14.6 us (2%)
    sub x3, other arithmetic, attend(): exp_terms = jnp.exp(scores - row_peak)  152 us
    ppermute x7, waiting for transfers between devices, shards(): lax.ppermute(ring[-1], 'tp', [(dev, (dev + 1) % 8) for dev in range(8)])  106 us
    reduce_scatter x1, waiting for transfers between devices, shards(): lax.psum_scatter(jnp.dot(block_rows, wo_full, preferred_element_type=jnp....  76.5 us
    reduce_scatter x1, waiting for transfers between devices, shards(): lax.psum_scatter(jnp.dot(block_rows, down_full, preferred_element_type=jn...  70.2 us
    all_gather x1, waiting for transfers between devices, shards(): gate_sum = add_single(lax.all_gather(gate_weight, 'sp', axis=0, tiled=True))  67.3 us
    dot_general x4, matrix products, attend(): jnp.einsum('hgqk,khd->qhgd', probs, v_three, preferred_element_type=jnp.f...  37.6 us
    dot_general x3, matrix products, attend(): jnp.einsum('qhgd,khd->hgqk', q_four, k_three, preferred_element_type=jnp....  36.4 us
    broadcast_in_dim x4, local copies, waits for them, and re-layouts, attend(): scores = jnp.where(causal[None, None, :, :], scores, -1e+30)  30 us
  transfers between devices with their start and end apart: 16, of which 12 were waited for; matrix products, arithmetic and copies ran while one was open for 47% of the time, Pallas kernels for 0%

profile of v1, /device:TPU:0, one launch (start us, length us, event | category | flops | bytes accessed | tf_op | source)
XLA Modules:
  0.0 822.1 jit_solution(10945971961109001587)
XLA Ops:
  8.5 20.7 %all_to_all.48 = bf16[256,4,256]{0,2,1:T(8,128)(2,1)} all-to-all(bf16[256,4,256]{0,2,1:T(8,128)(2,1)S(1)} %bitcast.107), channel_id=1, replica_groups=mesh['sp'=4,'tp'=8] {'sp'}, dimensions={1} | all-to-all | bytes 1048576 | tf_op jit(solution)/shard_map/all_to_all | solution.py:42
  30.4 16.8 %all_to_all.49 = bf16[256,4,256]{2,0,1:T(8,128)(2,1)} all-to-all(bf16[256,4,256]{2,0,1:T(8,128)(2,1)S(1)} %bitcast.108), channel_id=1, replica_groups=mesh['sp'=4,'tp'=8] {'sp'}, dimensions={1} | all-to-all | bytes 1048576 | tf_op jit(solution)/shard_map/all_to_all | solution.py:43
  64.1 13.6 %all-to-all-done.1 = bf16[256,4,512]{0,2,1:T(8,128)(2,1)S(1)} async-done(((bf16[256,4,512]{0,2,1:T(8,128)(2,1)}), bf16[256,4,512]{0,2,1:T(8,128)(2,1)S(1)}, u32[]{:S(2)}, u32[]{:S(2)}) %all-to-all-start.1) | async-done | bytes 1048608 | tf_op jit(solution)/shard_map/all_to_all | solution.py:40
  124.1 18.2 %fusion.19 = f32[2,8192,256,2]{2,1,3,0:T(8,128)} fusion(bf16[256,2,2,128]{0,3,2,1:T(8,128)(2,1)} %bitcast.111, bf16[8192,2,128,1]{2,1,0,3:T(2,128)(2,1)} %bitcast.98), kind=kOutput, calls=%fused_computation.34 | convolution fusion | flops 2147483648 | bytes 38010880 | tf_op jit(solution)/shard_map/qhgd,khd->hgqk/dot_general | solution.py:16
  160.5 18.2 %fusion.82 = (f32[2,2,256]{2,1,0:T(2,128)S(1)}, f32[2,2,256,4096]{2,3,1,0:T(8,128)}) fusion(f32[2,4096,256,2]{2,1,3,0:T(8,128)} %fusion.38, pred[256,4096]{0,1:T(8,128)(4,1)S(1)} %copy-done.12), kind=kOutput, calls=%fused_computation.118 | output fusion | flops 25169920 | bytes 34607104 | tf_op jit(solution)/shard_map/sub | solution.py:22
  181.8 10.5 %broadcast_in_dim.53 = f32[2,2,256,6144]{2,3,1,0:T(8,128)} broadcast(f32[]{:T(128)} %constant.69.clone.1), dimensions={} | broadcast | bytes 25165828 | tf_op jit(solution)/shard_map/jit(_where)/broadcast_in_dim | solution.py:20
  202.7 56.0 %fusion.81 = (f32[2,2,256]{2,1,0:T(2,128)S(1)}, f32[2,2,256,6144]{2,3,1,0:T(8,128)}) fusion(pred[2,2,256,6144]{2,3,1,0:T(8,128)(4,1)S(1)} %broadcast_in_dim.52, f32[2,2,256,6144]{2,3,1,0:T(8,128)} %broadcast_in_dim.53, f32[2,6144,256,2]{2,1,3,0:T(8,128)} %fusion.31, f32[2,6144,256,2]{2,1,3,0:T(8,128)} %mul.83), kind=kOutput, calls=%fused_computation.117 | output fusion | flops 37754880 | bytes 106958848 | tf_op jit(solution)/shard_map/sub | solution.py:22
  258.8 11.8 %fusion.44 = bf16[2,2,256,128]{2,3,1,0:T(8,128)(2,1)} fusion(f32[2,2,256,6144]{2,3,1,0:T(8,128)} %get-tuple-element.15, f32[2,2,256]{2,1,0:T(2,128)S(1)} %get-tuple-element.14, bf16[6144,2,128,1]{2,1,0,3:T(2,128)(2,1)} %bitcast.103), kind=kOutput, calls=%fused_computation.60 | convolution fusion | flops 1623326720 | bytes 28577792 | tf_op jit(solution)/shard_map/hgqk,khd->qhgd/dot_general | solution.py:24
  290.4 11.1 %broadcast_in_dim.77 = f32[2,2,256,8192]{2,3,1,0:T(8,128)} broadcast(f32[]{:T(128)} %constant.69.clone.1), dimensions={} | broadcast | bytes 33554436 | tf_op jit(solution)/shard_map/jit(_where)/broadcast_in_dim | solution.py:20
  301.5 11.0 %mul.86 = f32[2,8192,256,2]{2,1,3,0:T(8,128)} broadcast(f32[]{:T(128)} %constant.68.clone.1), dimensions={} | broadcast | bytes 33554436 | tf_op jit(solution)/shard_map/mul | solution.py:16
  312.5 78.0 %fusion.80 = (f32[2,2,256]{2,1,0:T(2,128)S(1)}, f32[2,2,256,8192]{2,3,1,0:T(8,128)}) fusion(pred[2,2,256,8192]{2,3,1,0:T(8,128)(4,1)} %broadcast_in_dim.76, f32[2,2,256,8192]{2,3,1,0:T(8,128)} %broadcast_in_dim.77, f32[2,8192,256,2]{2,1,3,0:T(8,128)} %fusion.19, f32[2,8192,256,2]{2,1,3,0:T(8,128)} %mul.86), kind=kOutput, calls=%fused_computation.116 | output fusion | flops 50339840 | bytes 142610432 | tf_op jit(solution)/shard_map/sub | solution.py:22
  401.5 13.5 %fusion.47 = bf16[2,2,256,128]{2,3,1,0:T(8,128)(2,1)S(1)} fusion(f32[2,2,256,8192]{2,3,1,0:T(8,128)} %get-tuple-element.13, f32[2,2,256]{2,1,0:T(2,128)S(1)} %get-tuple-element.12, bf16[8192,2,128,1]{2,1,0,3:T(2,128)(2,1)} %bitcast.101), kind=kOutput, calls=%fused_computation.61 | convolution fusion | flops 2164391936 | bytes 38014976 | tf_op jit(solution)/shard_map/hgqk,khd->qhgd/dot_general | solution.py:24
  421.8 76.5 %reduce-scatter.3.cloned.1.call-done = bf16[256,2048]{1,0:T(8,128)(2,1)} async-done(((bf16[1024,2048]{1,0:T(8,128)(2,1)}), bf16[256,2048]{1,0:T(8,128)(2,1)}) %reduce-scatter.3.cloned.1.call-update) | async-done | bytes 1048592 | tf_op jit(solution)/shard_map/reduce_scatter | solution.py:79
  500.5 15.1 %collective-permute-done = bf16[256,2048]{1,0:T(8,128)(2,1)S(1)} collective-permute-done((bf16[256,2048]{1,0:T(8,128)(2,1)S(1)}, bf16[256,2048]{1,0:T(8,128)(2,1)S(1)}, u32[]{:S(2)}, u32[]{:S(2)}) %collective-permute-start) | collective-permute-done | bytes 1048608 | tf_op jit(solution)/shard_map/ppermute | solution.py:93
  515.7 15.0 %collective-permute-done.1 = bf16[256,2048]{1,0:T(8,128)(2,1)S(1)} collective-permute-done((bf16[256,2048]{1,0:T(8,128)(2,1)S(1)}, bf16[256,2048]{1,0:T(8,128)(2,1)S(1)}, u32[]{:S(2)}, u32[]{:S(2)}) %collective-permute-start.1) | collective-permute-done | bytes 1048608 | tf_op jit(solution)/shard_map/ppermute | solution.py:93
  530.7 15.1 %collective-permute-done.2 = bf16[256,2048]{1,0:T(8,128)(2,1)S(1)} collective-permute-done((bf16[256,2048]{1,0:T(8,128)(2,1)S(1)}, bf16[256,2048]{1,0:T(8,128)(2,1)S(1)}, u32[]{:S(2)}, u32[]{:S(2)}) %collective-permute-start.2) | collective-permute-done | bytes 1048608 | tf_op jit(solution)/shard_map/ppermute | solution.py:93
  546.8 15.1 %collective-permute-done.3 = bf16[256,2048]{1,0:T(8,128)(2,1)S(1)} collective-permute-done((bf16[256,2048]{1,0:T(8,128)(2,1)S(1)}, bf16[256,2048]{1,0:T(8,128)(2,1)S(1)}, u32[]{:S(2)}, u32[]{:S(2)}) %collective-permute-start.3) | collective-permute-done | bytes 1048608 | tf_op jit(solution)/shard_map/ppermute | solution.py:93
  562.9 15.1 %collective-permute-done.4 = bf16[256,2048]{1,0:T(8,128)(2,1)S(1)} collective-permute-done((bf16[256,2048]{1,0:T(8,128)(2,1)S(1)}, bf16[256,2048]{1,0:T(8,128)(2,1)S(1)}, u32[]{:S(2)}, u32[]{:S(2)}) %collective-permute-start.4) | collective-permute-done | bytes 1048608 | tf_op jit(solution)/shard_map/ppermute | solution.py:93
  579.0 15.2 %collective-permute-done.5 = bf16[256,2048]{1,0:T(8,128)(2,1)} collective-permute-done((bf16[256,2048]{1,0:T(8,128)(2,1)S(1)}, bf16[256,2048]{1,0:T(8,128)(2,1)}, u32[]{:S(2)}, u32[]{:S(2)}) %collective-permute-start.5) | collective-permute-done | bytes 1048608 | tf_op jit(solution)/shard_map/ppermute | solution.py:93
  594.4 15.3 %collective-permute-done.6 = bf16[256,2048]{1,0:T(8,128)(2,1)} collective-permute-done((bf16[256,2048]{1,0:T(8,128)(2,1)}, bf16[256,2048]{1,0:T(8,128)(2,1)}, u32[]{:S(2)}, u32[]{:S(2)}) %collective-permute-start.6) | collective-permute-done | bytes 1048608 | tf_op jit(solution)/shard_map/ppermute | solution.py:93
  635.2 14.3 %fusion.13 = f32[2048,896]{1,0:T(8,128)} fusion(bf16[2048,896]{1,0:T(8,128)(2,1)} %all-gather.15.cloned.1.call-done, bf16[4096,2048]{1,0:T(8,128)(2,1)} %constant_dynamic-update-slice_fusion, s32[]{:T(128)S(6)} %select_n.47), kind=kOutput, calls=%fused_computation.27 | convolution fusion | flops 7516192768 | bytes 19398660 | tf_op jit(solution)/shard_map/dot_general | solution.py:29
  649.5 67.3 %all-gather.13.cloned.1.call-done = bf16[2048,896]{1,0:T(8,128)(2,1)} async-done(((bf16[512,896]{1,0:T(8,128)(2,1)}), bf16[2048,896]{1,0:T(8,128)(2,1)}) %all-gather.13.cloned.1.call-update) | async-done | bytes 3670032 | tf_op jit(solution)/shard_map/all_gather | solution.py:101
  716.8 25.5 %convolution_convert_fusion = bf16[2048,2048]{1,0:T(8,128)(2,1)} fusion(bf16[896,2048]{1,0:T(8,128)(2,1)} %all-gather.17.cloned.1.call-done, f32[2048,896]{1,0:T(8,128)} %fusion.13, bf16[2048,896]{1,0:T(8,128)(2,1)} %all-gather.13.cloned.1.call-done, bf16[4096,2048]{1,0:T(8,128)(2,1)} %constant_dynamic-update-slice_fusion, s32[]{:T(128)S(6)} %select_n.47), kind=kOutput, calls=%fused_computation.26 | convolution fusion | flops 15047589888 | bytes 31457284 | tf_op jit(solution)/shard_map/dot_general | solution.py:107
  742.3 70.2 %reduce-scatter.5.cloned.1.call-done = bf16[256,2048]{1,0:T(8,128)(2,1)} async-done(((bf16[2048,2048]{1,0:T(8,128)(2,1)}), bf16[256,2048]{1,0:T(8,128)(2,1)}) %reduce-scatter.5.cloned.1.call-update) | async-done | bytes 1048592 | tf_op jit(solution)/shard_map/reduce_scatter | solution.py:106
  (131 shorter events, 168.2 us)
Async XLA Ops:
  7.2 71.5 %all-gather.7.cloned.1.call-start = ((), (), s32[]{:S(2)}) async-start(), calls=%async_computation.5 | async-start | bytes 4718592 | tf_op jit(solution)/shard_map/all_gather | solution.py:47
  29.2 75.1 %all-gather.9.cloned.1.call-start = ((), (), s32[]{:S(2)}) async-start(), calls=%async_computation.6 | async-start | bytes 4718592 | tf_op jit(solution)/shard_map/all_gather | solution.py:48
  49.4 28.3 %all-to-all-start.1 = ((bf16[256,4,512]{0,2,1:T(8,128)(2,1)}), bf16[256,4,512]{0,2,1:T(8,128)(2,1)S(1)}, u32[]{:S(2)}, u32[]{:S(2)}) async-start(bf16[256,4,512]{0,2,1:T(8,128)(2,1)} %bitcast.4), calls=%async_computation.1 | async-start | bytes 2097152 | tf_op jit(solution)/shard_map/all_to_all | solution.py:40
  53.0 362.1 %all-gather.11.cloned.1.call-start = ((), (), s32[]{:S(2)}) async-start(), calls=%async_computation.7 | async-start | bytes 2359296 | tf_op jit(solution)/shard_map/all_gather | solution.py:77
  53.7 444.6 %reduce-scatter.3.cloned.1.call-start = ((), (), s32[]{:S(2)}) async-start(), calls=%async_computation.8 | async-start | bytes 5242880 | tf_op jit(solution)/shard_map/reduce_scatter | solution.py:79
  124.1 18.2 %copy-start.1 = (bf16[6144,2,128]{2,1,0:T(2,128)(2,1)S(1)}, bf16[6144,2,128]{2,1,0:T(2,128)(2,1)}, u32[]{:S(2)}) copy-start(bf16[6144,2,128]{2,1,0:T(2,128)(2,1)} %reshape.205) | copy-start | bytes 9437188
  124.1 18.2 %copy-start.11 = (bf16[1,256,512]{1,2,0:T(8,128)(2,1)S(1)}, bf16[1,256,512]{1,2,0:T(8,128)(2,1)}, u32[]{:S(2)}) copy-start(bf16[1,256,512]{1,2,0:T(8,128)(2,1)} %get-tuple-element.6) | copy-start | bytes 786436
  312.5 78.0 %copy-start.14 = (bf16[1,2048,256]{1,2,0:T(8,128)(2,1)S(1)}, bf16[1,2048,256]{1,2,0:T(8,128)(2,1)}, u32[]{:S(2)}) copy-start(bf16[1,2048,256]{1,2,0:T(8,128)(2,1)} %copy.24) | copy-start | bytes 3145732
  401.5 13.6 %copy-start.18 = (bf16[2,2,256,128]{2,3,1,0:T(8,128)(2,1)S(1)}, bf16[2,2,256,128]{2,3,1,0:T(8,128)(2,1)}, u32[]{:S(2)}) copy-start(bf16[2,2,256,128]{2,3,1,0:T(8,128)(2,1)} %fusion.41) | copy-start | bytes 786436
  415.1 83.2 %copy-start.13 = (bf16[256,2048]{1,0:T(8,128)(2,1)S(1)}, bf16[256,2048]{1,0:T(8,128)(2,1)}, u32[]{:S(2)}) copy-start(bf16[256,2048]{1,0:T(8,128)(2,1)} %param.9) | copy-start | bytes 3145732
  421.2 214.0 %all-gather.15.cloned.1.call-start = ((), (), s32[]{:S(2)}) async-start(), calls=%async_computation.10 | async-start | bytes 4587520 | tf_op jit(solution)/shard_map/all_gather | solution.py:102
  421.8 227.7 %all-gather.17.cloned.1.call-start = ((), (), s32[]{:S(2)}) async-start(), calls=%async_computation.11 | async-start | bytes 4587520 | tf_op jit(solution)/shard_map/all_gather | solution.py:104
  500.1 312.4 %copy-start = (bf16[256,2048]{1,0:T(8,128)(2,1)}, bf16[256,2048]{1,0:T(8,128)(2,1)S(1)}, u32[]{:S(2)}) copy-start(bf16[256,2048]{1,0:T(8,128)(2,1)S(1)} %get-tuple-element.3) | copy-start | bytes 3145732
  500.4 15.2 %collective-permute-start = (bf16[256,2048]{1,0:T(8,128)(2,1)S(1)}, bf16[256,2048]{1,0:T(8,128)(2,1)S(1)}, u32[]{:S(2)}, u32[]{:S(2)}) collective-permute-start(bf16[256,2048]{1,0:T(8,128)(2,1)S(1)} %fusion.35), channel_id=1, source_target_pairs={{0,1},{1,2},{2,3},{3,4},{4,5},{5,6},{6,7},{7,0},{8,9},{9,10},{10,1... | collective-permute-start | bytes 3145736 | tf_op jit(solution)/shard_map/ppermute | solution.py:93
  515.6 15.1 %collective-permute-start.1 = (bf16[256,2048]{1,0:T(8,128)(2,1)S(1)}, bf16[256,2048]{1,0:T(8,128)(2,1)S(1)}, u32[]{:S(2)}, u32[]{:S(2)}) collective-permute-start(bf16[256,2048]{1,0:T(8,128)(2,1)S(1)} %collective-permute-done), channel_id=1, source_target_pairs={{0,1},{1,2},{2,3},{3,4},{4,5},{5,6},{6,7},{7,0},{8,9},{9,10},{10,1... | collective-permute-start | bytes 3145736 | tf_op jit(solution)/shard_map/ppermute | solution.py:93
  515.6 201.2 %all-gather.13.cloned.1.call-start = ((), (), s32[]{:S(2)}) async-start(), calls=%async_computation.9 | async-start | bytes 4587520 | tf_op jit(solution)/shard_map/all_gather | solution.py:101
  530.7 15.1 %collective-permute-start.2 = (bf16[256,2048]{1,0:T(8,128)(2,1)S(1)}, bf16[256,2048]{1,0:T(8,128)(2,1)S(1)}, u32[]{:S(2)}, u32[]{:S(2)}) collective-permute-start(bf16[256,2048]{1,0:T(8,128)(2,1)S(1)} %collective-permute-done.1), channel_id=1, source_target_pairs={{0,1},{1,2},{2,3},{3,4},{4,5},{5,6},{6,7},{7,0},{8,9},{9,10},{10,1... | collective-permute-start | bytes 3145736 | tf_op jit(solution)/shard_map/ppermute | solution.py:93
  546.8 15.1 %collective-permute-start.3 = (bf16[256,2048]{1,0:T(8,128)(2,1)S(1)}, bf16[256,2048]{1,0:T(8,128)(2,1)S(1)}, u32[]{:S(2)}, u32[]{:S(2)}) collective-permute-start(bf16[256,2048]{1,0:T(8,128)(2,1)S(1)} %collective-permute-done.2), channel_id=1, source_target_pairs={{0,1},{1,2},{2,3},{3,4},{4,5},{5,6},{6,7},{7,0},{8,9},{9,10},{10,1... | collective-permute-start | bytes 3145736 | tf_op jit(solution)/shard_map/ppermute | solution.py:93
  562.9 15.1 %collective-permute-start.4 = (bf16[256,2048]{1,0:T(8,128)(2,1)S(1)}, bf16[256,2048]{1,0:T(8,128)(2,1)S(1)}, u32[]{:S(2)}, u32[]{:S(2)}) collective-permute-start(bf16[256,2048]{1,0:T(8,128)(2,1)S(1)} %collective-permute-done.3), channel_id=1, source_target_pairs={{0,1},{1,2},{2,3},{3,4},{4,5},{5,6},{6,7},{7,0},{8,9},{9,10},{10,1... | collective-permute-start | bytes 3145736 | tf_op jit(solution)/shard_map/ppermute | solution.py:93
  579.0 15.2 %collective-permute-start.5 = (bf16[256,2048]{1,0:T(8,128)(2,1)S(1)}, bf16[256,2048]{1,0:T(8,128)(2,1)}, u32[]{:S(2)}, u32[]{:S(2)}) collective-permute-start(bf16[256,2048]{1,0:T(8,128)(2,1)S(1)} %collective-permute-done.4), channel_id=1, source_target_pairs={{0,1},{1,2},{2,3},{3,4},{4,5},{5,6},{6,7},{7,0},{8,9},{9,10},{10,1... | collective-permute-start | bytes 3145736 | tf_op jit(solution)/shard_map/ppermute | solution.py:93
  594.3 15.4 %collective-permute-start.6 = (bf16[256,2048]{1,0:T(8,128)(2,1)}, bf16[256,2048]{1,0:T(8,128)(2,1)}, u32[]{:S(2)}, u32[]{:S(2)}) collective-permute-start(bf16[256,2048]{1,0:T(8,128)(2,1)} %collective-permute-done.5), channel_id=1, source_target_pairs={{0,1},{1,2},{2,3},{3,4},{4,5},{5,6},{6,7},{7,0},{8,9},{9,10},{10,1... | collective-permute-start | bytes 3145736 | tf_op jit(solution)/shard_map/ppermute | solution.py:93
  594.3 218.2 %reduce-scatter.5.cloned.1.call-start = ((), (), s32[]{:S(2)}) async-start(), calls=%async_computation.12 | async-start | bytes 9437184 | tf_op jit(solution)/shard_map/reduce_scatter | solution.py:106
  594.4 24.8 %copy-start.5 = (bf16[256,2048]{1,0:T(8,128)(2,1)S(1)}, bf16[256,2048]{1,0:T(8,128)(2,1)}, u32[]{:S(2)}) copy-start(bf16[256,2048]{1,0:T(8,128)(2,1)} %copy-done.4) | copy-start | bytes 3145732
  614.3 14.1 %copy-start.9 = (bf16[256,2048]{1,0:T(8,128)(2,1)S(1)}, bf16[256,2048]{1,0:T(8,128)(2,1)}, u32[]{:S(2)}) copy-start(bf16[256,2048]{1,0:T(8,128)(2,1)} %copy-done.8) | copy-start | bytes 3145732
  (16 other events, 115.2 us)
Sparse Core Ops, SparseCore 0:
  29.3 36.4 all-gather.6
  67.7 36.5 all-gather.8
  106.2 28.0 all-gather.10
  421.3 77.0 reduce-scatter.2
  499.8 72.5 all-gather.14
  573.8 70.6 all-gather.16
  646.1 70.6 all-gather.12
  742.4 70.0 reduce-scatter.4
